TPU v7x, 32 devices: a whole 2x2x4 slice. The times are simulated.
32 devices in a mesh: seq: 8 (over z, x), head: 4 (over y, core).
Axes of the slice: x: 2, y: 2, z: 4, core: 2. Of those that a mesh axis runs over, the one named last changes fastest.
Arguments:
- queries: bfloat16 [8192, 4096], P('seq', 'head'), may hold values from -8 to 8
- key_rows: bfloat16 [8192, 4096], P('seq', 'head'), may hold values from -8 to 8
- value_rows: bfloat16 [8192, 4096], P('seq', 'head'), may hold values from -6 to 6
- random_owner: int32 [128, 3], P('seq'), may hold values from 0 to 7, all different within a row; in each aligned block of 16 rows (0 to 15, 16 to 31, ...) at most 8 rows name the same one
- random_local: int32 [128, 3], P('seq'), may hold values from 0 to 15
- output_weight: bfloat16 [4096, 4096], P('head'), may hold values from -0.09375 to 0.09375
Outputs:
- layer_output: bfloat16 [8192, 4096], P(('seq', 'head'))
Inputs may be any that keep to these rules, and one draw needn't show every extreme that they name: `random_owner`: each row names 3 different owners. Among the rows of one device (16 aligned rows) no owner is named more than 8 times, and in some device's rows one owner is named exactly 8 times.
All inputs are finite; a program needn't handle non-finite values.
Results may differ from a plain program's by a relative error of at most 0.0052.
Values may be sent and summed in bfloat16 or wider, within the bound.
No kernel may reach another device: no remote copies, remote signals or barrier semaphores. Data moves between devices by JAX's collectives and lax.ppermute only.
A program may use at most 192 MiB of HBM per device.

v0:
```python
import math
import jax
import jax.numpy as jnp
from jax import lax
from jax.sharding import PartitionSpec as P

HEAD_DIM = 128
BLOCK = 64
RANDOM = 3
GLOBAL = 128
masked_score = -1e30


def padded(array, sides, width):
    for axis, dim in sides:
        peers, length = (lax.axis_size(axis), array.shape[dim])
        up = [(i, (i + 1) % peers) for i in range(peers - 1)]
        down = [(j, i) for i, j in up]
        last = lax.slice_in_dim(array, length - width, length, axis=dim)
        first = lax.slice_in_dim(array, 0, width, axis=dim)
        before = lax.ppermute(last, axis, up)
        after = lax.ppermute(first, axis, down)
        array = jnp.concatenate([before, array, after], axis=dim)
    return array


def from_root(block, axis, holder):
    block = jnp.where(lax.axis_index(axis) == holder, block, jnp.zeros_like(block))
    return lax.psum(block, axis)


def combined_all(array, axis, combine):
    everything = jax.tree.map(lambda part: lax.all_gather(part, axis), array)
    first = jax.tree.map(lambda part: part[0], everything)

    def lap(k, so_far):
        return combine(so_far, jax.tree.map(lambda part: part[k], everything))

    return lax.fori_loop(1, lax.axis_size(axis), lap, first)


def slot_table(owner_ids, local_ids, seq_count, slot_count):
    owner_hits = (owner_ids[:, None] == jnp.arange(seq_count, dtype=jnp.int32)[None, :]).astype(
        jnp.int32
    )
    earlier = jnp.cumsum(owner_hits, axis=0) - owner_hits
    slot_ids = jnp.sum(earlier * owner_hits, axis=1)
    slot_hits = (slot_ids[:, None] == jnp.arange(slot_count, dtype=jnp.int32)[None, :]).astype(
        jnp.int32
    )
    request_table = jnp.sum(
        (owner_hits * local_ids[:, None])[:, :, None] * slot_hits[:, None, :], axis=0
    )
    return (request_table, slot_ids)


def local(queries, key_rows, value_rows, random_owner, random_local, output_weight):
    seq_count = lax.axis_size("seq")
    seq_index = lax.axis_index("seq")
    token_count, width_here = queries.shape
    blocks_here = token_count // BLOCK
    heads_here = width_here // HEAD_DIM
    slot_count = max(2, 4 * blocks_here // seq_count)
    total_blocks = seq_count * blocks_here
    score_scale = HEAD_DIM ** (-0.5)
    key_blocks = key_rows.reshape(blocks_here, BLOCK, width_here)
    value_blocks = value_rows.reshape(blocks_here, BLOCK, width_here)
    edge_slots = 0
    owner_flat = random_owner.reshape(-1)
    local_flat = random_local.reshape(-1)
    request_table, slot_ids = slot_table(owner_flat, local_flat, seq_count, slot_count)
    wanted = lax.all_to_all(request_table, "seq", split_axis=0, concat_axis=0, tiled=True)
    sent_keys = jnp.take(key_blocks, wanted, axis=0)
    sent_values = jnp.take(value_blocks, wanted, axis=0)
    got_keys = lax.all_to_all(sent_keys, "seq", split_axis=0, concat_axis=0, tiled=True)
    got_values = lax.all_to_all(sent_values, "seq", split_axis=0, concat_axis=0, tiled=True)
    slot_width = slot_count + edge_slots
    flat_slots = owner_flat * slot_width + slot_ids
    random_keys = jnp.take(got_keys.reshape(-1, BLOCK, width_here), flat_slots, axis=0)
    random_values = jnp.take(got_values.reshape(-1, BLOCK, width_here), flat_slots, axis=0)
    edge_pairs = jnp.stack(
        [jnp.stack([key_blocks[0], value_blocks[0]]), jnp.stack([key_blocks[-1], value_blocks[-1]])]
    )
    widened = padded(edge_pairs, (("seq", 0),), 1)
    left_key, left_value = (widened[0, 0], widened[0, 1])
    right_key, right_value = (widened[3, 0], widened[3, 1])
    global_rows = jnp.stack([queries[:GLOBAL], key_rows[:GLOBAL], value_rows[:GLOBAL]])
    global_rows = from_root(global_rows, "seq", 0)
    global_query = global_rows[0].reshape(GLOBAL, heads_here, HEAD_DIM)
    key_heads = key_rows.reshape(token_count, heads_here, HEAD_DIM)
    value_heads = value_rows.reshape(token_count, heads_here, HEAD_DIM)
    scores = (
        jnp.einsum("qhd,khd->hqk", global_query, key_heads, preferred_element_type=jnp.float32)
        * score_scale
    )
    row_max = jnp.max(scores, axis=2)
    weight = jnp.exp(scores - row_max[:, :, None])
    row_total = jnp.sum(weight, axis=2)
    partial_value = jnp.einsum(
        "hqk,khd->hqd", weight.astype(jnp.bfloat16), value_heads, preferred_element_type=jnp.float32
    )

    def combine(left_part, right_part):
        joint_max = jnp.maximum(left_part[0], right_part[0])
        left_factor = jnp.exp(left_part[0] - joint_max)
        right_factor = jnp.exp(right_part[0] - joint_max)
        return (
            joint_max,
            left_part[1] * left_factor + right_part[1] * right_factor,
            left_part[2] * left_factor[:, :, None] + right_part[2] * right_factor[:, :, None],
        )

    row_max, row_total, partial_value = combined_all(
        (row_max, row_total, partial_value), "seq", combine
    )
    global_out = jnp.transpose(partial_value / row_total[:, :, None], (1, 0, 2)).reshape(
        GLOBAL, width_here
    )
    key_padded = jnp.concatenate([left_key[None], key_blocks, right_key[None]], axis=0)
    value_padded = jnp.concatenate([left_value[None], value_blocks, right_value[None]], axis=0)
    global_keys = global_rows[1].reshape(GLOBAL // BLOCK, BLOCK, width_here)
    global_values = global_rows[2].reshape(GLOBAL // BLOCK, BLOCK, width_here)
    group_size = math.gcd(blocks_here, max(1, 512 // BLOCK))
    group_count = blocks_here // group_size
    listed = (3 + RANDOM) * BLOCK + GLOBAL
    slot_number = jnp.arange(listed, dtype=jnp.int32) // BLOCK

    def attend(packed):
        number, query_group, key_group, value_group = packed
        block_ids = (
            seq_index * blocks_here + number * group_size + jnp.arange(group_size, dtype=jnp.int32)
        )
        near_keys = lax.dynamic_slice_in_dim(key_padded, number * group_size, group_size + 2, 0)
        near_values = lax.dynamic_slice_in_dim(value_padded, number * group_size, group_size + 2, 0)
        window_keys = jnp.stack([near_keys[:-2], near_keys[1:-1], near_keys[2:]], axis=1)
        window_values = jnp.stack([near_values[:-2], near_values[1:-1], near_values[2:]], axis=1)
        listed_keys = jnp.concatenate(
            [
                window_keys,
                key_group,
                jnp.broadcast_to(global_keys[None], (group_size,) + global_keys.shape),
            ],
            axis=1,
        )
        listed_values = jnp.concatenate(
            [
                window_values,
                value_group,
                jnp.broadcast_to(global_values[None], (group_size,) + global_values.shape),
            ],
            axis=1,
        )
        group_keys = listed_keys.reshape(group_size, listed, heads_here, HEAD_DIM)
        group_values = listed_values.reshape(group_size, listed, heads_here, HEAD_DIM)
        query_heads = query_group.reshape(group_size, BLOCK, heads_here, HEAD_DIM)
        block_scores = (
            jnp.einsum(
                "bqhd,bkhd->bhqk", query_heads, group_keys, preferred_element_type=jnp.float32
            )
            * score_scale
        )
        usable = jnp.logical_and(
            jnp.logical_or(slot_number[None, :] != 0, block_ids[:, None] > 0),
            jnp.logical_or(slot_number[None, :] != 2, block_ids[:, None] < total_blocks - 1),
        )
        usable_keys = usable[:, None, None, :]
        block_scores = jnp.where(usable_keys, block_scores, masked_score)
        block_max = jnp.max(block_scores, axis=3, keepdims=True)
        block_weight = jnp.where(usable_keys, jnp.exp(block_scores - block_max), 0.0)
        block_total = jnp.sum(block_weight, axis=3)
        context = jnp.einsum(
            "bhqk,bkhd->bqhd",
            block_weight.astype(jnp.bfloat16),
            group_values,
            preferred_element_type=jnp.float32,
        )
        context = context / jnp.transpose(block_total, (0, 2, 1))[:, :, :, None]
        return context.reshape(group_size * BLOCK, width_here).astype(jnp.bfloat16)

    numbers = jnp.arange(group_count, dtype=jnp.int32)
    query_groups = queries.reshape(group_count, group_size, BLOCK, width_here)
    random_key_groups = random_keys.reshape(group_count, group_size, RANDOM, BLOCK, width_here)
    random_value_groups = random_values.reshape(group_count, group_size, RANDOM, BLOCK, width_here)
    sparse = lax.map(
        attend, (numbers, query_groups, random_key_groups, random_value_groups)
    ).reshape(token_count, width_here)
    top_rows = jnp.where(seq_index == 0, global_out.astype(jnp.bfloat16), sparse[:GLOBAL])
    attention = jnp.concatenate([top_rows, sparse[GLOBAL:]], axis=0)
    summed = lax.psum_scatter(
        jnp.dot(attention, output_weight, preferred_element_type=jnp.float32),
        "head",
        scatter_dimension=0,
        tiled=True,
    )
    return summed.astype(jnp.bfloat16)


def solution(mesh):
    in_specs = (
        P("seq", "head"),
        P("seq", "head"),
        P("seq", "head"),
        P("seq", None),
        P("seq", None),
        P("head", None),
    )
    out_specs = P(("seq", "head"), None)
    return jax.shard_map(local, mesh=mesh, in_specs=in_specs, out_specs=out_specs, check_vma=False)
```

profile of v0, /device:TPU:0, one launch (start us, length us, event | category | flops | bytes accessed | tf_op | source)
XLA Modules:
  0.0 904.8 jit_solution(16662353208190921498)
XLA Ops:
  8.9 13.6 %all_to_all.22 = s32[8,1,8]{2,1,0:T(1,128)S(1)} all-to-all(s32[8,1,8]{2,1,0:T(1,128)S(1)} %bitcast.212), channel_id=1, replica_groups=mesh['seq'=8,'head'=4] {'seq'}, dimensions={0} | all-to-all | bytes 512 | tf_op jit(solution)/shard_map/all_to_all | solution.py:72
  22.6 7.2 gather_fusion
  29.8 5.5 gather_fusion.2
  35.3 9.4 %broadcast_select_fusion = (bf16[8,8,64,1024]{3,2,1,0:T(8,128)(2,1)}, bf16[8,8,64,1024]{3,2,1,0:T(8,128)(2,1)S(1)}) fusion(bf16[8,8,64,1024]{3,2,1,0:T(8,128)(2,1)} %bitcast.198, pred[8,8]{1,0:T(8,128)(4,1)S(1)} %compare_and_fusion, bf16[8,8,64,1024]{3,2,1,0:T(8,128)(2,1)} %bitcast.197), kind=kLoop, calls=%fused_computation.61 | loop fusion | flops 8388608 | bytes 33554496 | tf_op jit(solution)/shard_map/jit(_take)/select_n | solution.py:73
  44.7 185.8 %all_to_all.23 = bf16[8,8,64,1024]{3,2,1,0:T(8,128)(2,1)} all-to-all(bf16[8,8,64,1024]{3,2,1,0:T(8,128)(2,1)S(1)} %get-tuple-element.475), channel_id=1, replica_groups=mesh['seq'=8,'head'=4] {'seq'}, dimensions={0} | all-to-all | bytes 16777216 | tf_op jit(solution)/shard_map/all_to_all | solution.py:76
  230.5 5.2 all-to-all-start.2
  238.3 228.5 %all-reduce.2.cloned.1.call-done = bf16[3,128,1024]{1,2,0:T(8,128)(2,1)} async-done(((bf16[3,128,1024]{1,2,0:T(8,128)(2,1)}), bf16[3,128,1024]{1,2,0:T(8,128)(2,1)}) %all-reduce.2.cloned.1.call-update) | async-done | bytes 786448 | tf_op jit(solution)/shard_map/psum | solution.py:29
  469.0 1.9 copy-done.3
  470.9 2.1 fusion.38
  474.1 2.6 collective-permute-start
  478.1 11.4 %collective-permute-done = bf16[1,2,64,1024]{3,2,1,0:T(8,128)(2,1)S(1)} collective-permute-done((bf16[1,2,64,1024]{3,2,1,0:T(8,128)(2,1)S(1)}, bf16[1,2,64,1024]{3,2,1,0:T(8,128)(2,1)S(1)}, u32[]{:S(2)}, u32[]{:S(2)}) %collective-permute-start) | collective-permute-done | bytes 262176 | tf_op jit(solution)/shard_map/ppermute | solution.py:21
  490.4 1.9 pad_maximum_fusion
  492.3 1.7 pad_maximum_fusion.1
  494.9 33.3 %all-gather.1 = f32[64,128]{1,0:T(8,128)S(1)} all-gather(f32[8,128]{1,0:T(8,128)S(1)} %fusion.37), channel_id=3, replica_groups=mesh['seq'=8,'head'=4] {'seq'}, dimensions={0}, use_global_device_ids=true | all-gather | bytes 36864 | tf_op jit(solution)/shard_map/all_gather | solution.py:33
  528.2 31.3 %all-gather = f32[64,128]{1,0:T(8,128)S(1)} all-gather(f32[8,128]{1,0:T(8,128)S(1)} %get-tuple-element.480), channel_id=2, replica_groups=mesh['seq'=8,'head'=4] {'seq'}, dimensions={0}, use_global_device_ids=true | all-gather | bytes 36864 | tf_op jit(solution)/shard_map/all_gather | solution.py:33
  562.3 11.0 %while.33 = (s32[]{:T(128)}, f32[8,128]{1,0:T(8,128)S(1)}, f32[8,128]{1,0:T(8,128)S(1)}, f32[8,128,128]{2,1,0:T(8,128)S(1)}, f32[8,8,128]{2,1,0:T(8,128)S(1)}, /...) while((s32[]{:T(128)}, f32[8,128]{1,0:T(8,128)S(1)}, ...), condition=%wide.region_4.5_spmd, body=%wide.region_3.4_spmd.sunk | while | flops 399365 | bytes 1613975 | solution.py:39
  574.2 8.4 gather_fusion.1
  582.6 8.4 gather_fusion.3
  591.0 10.4 %broadcast_select_fusion.2 = (bf16[48,64,1024]{2,1,0:T(8,128)(2,1)}, bf16[48,64,1024]{2,1,0:T(8,128)(2,1)}) fusion(bf16[48,64,1024]{2,1,0:T(8,128)(2,1)} %gather_fusion.3, pred[48]{0:T(512)(128)(4,1)S(1)} %get-tuple-element.453, bf16[48,64,1024]{2,1,0:T(8,128)(2,1)} %gather_fusion.1), kind=kLoop, calls=%fused_computation.63 | loop fusion | flops 6291456 | bytes 25165872 | tf_op jit(solution)/shard_map/jit(_take)/select_n | solution.py:79
  601.4 146.4 %while.34 = (s32[]{:T(128)}, bf16[2,512,1024]{2,1,0:T(8,128)(2,1)}, s32[2]{0:T(128)S(1)}, bf16[18,64,1024]{2,1,0:T(8,128)(2,1)S(1)}, bf16[2,8,3,64,1024]{4,3,2,1...) while((s32[]{:T(128)}, bf16[2,512,1024]{2,1,0:T(8,128)(2,1)}, ...), condition=%wide.region_11.14_spmd.clone.clone, body=%wide.region_8.13_spmd.clone.clone.sunk | while | flops 1091585536 | bytes 126397792 | solution.py:184
  605.9 2.3 fusion.87
  608.1 2.3 fusion.88
  610.4 2.2 fusion.89
  612.6 6.7 bitcast_dynamic-update-slice_fusion.3
  619.3 2.5 broadcast_dynamic-update-slice_fusion.5
  621.8 8.9 copy.127
  631.2 9.6 %fusion.93 = f32[8,8,64,512]{3,2,1,0:T(8,128)} fusion(bf16[8,512,8,128]{3,2,1,0:T(8,128)(2,1)} %bitcast.186, bf16[8,64,8,128]{3,2,1,0:T(8,128)(2,1)S(1)} %bitcast.189), kind=kOutput, calls=%fused_computation.16.clone.1 | convolution fusion | flops 536870912 | bytes 17825792 | tf_op jit(solution)/shard_map/while/body/eval_jaxpr/bqhd,bkhd->bhqk/dot_general | solution.py:157
  640.9 11.5 %fusion.96 = (f32[8,8,64]{2,1,0:T(8,128)S(1)}, bf16[8,8,64,512]{3,2,1,0:T(8,128)(2,1)}) fusion(f32[8,8,64,512]{3,2,1,0:T(8,128)} %fusion.93, pred[8,512]{1,0:T(8,128)(4,1)S(1)} %or_and_fusion.2), kind=kOutput, calls=%fused_computation.111.clone.1 | output fusion | flops 16777728 | bytes 12603392 | tf_op jit(solution)/shard_map/while/body/eval_jaxpr/sub | solution.py:169
  652.4 2.5 broadcast_dynamic-update-slice_fusion.4
  654.9 8.8 copy.126
  663.7 6.6 fusion.97
  670.3 1.7 copy.129
  679.1 2.3 fusion.87
  681.3 2.3 fusion.88
  683.6 2.2 fusion.89
  685.8 6.7 bitcast_dynamic-update-slice_fusion.3
  692.5 2.5 broadcast_dynamic-update-slice_fusion.5
  695.0 8.9 copy.127
  704.4 9.6 %fusion.93 = f32[8,8,64,512]{3,2,1,0:T(8,128)} fusion(bf16[8,512,8,128]{3,2,1,0:T(8,128)(2,1)} %bitcast.186, bf16[8,64,8,128]{3,2,1,0:T(8,128)(2,1)S(1)} %bitcast.189), kind=kOutput, calls=%fused_computation.16.clone.1 | convolution fusion | flops 536870912 | bytes 17825792 | tf_op jit(solution)/shard_map/while/body/eval_jaxpr/bqhd,bkhd->bhqk/dot_general | solution.py:157
  714.1 11.5 %fusion.96 = (f32[8,8,64]{2,1,0:T(8,128)S(1)}, bf16[8,8,64,512]{3,2,1,0:T(8,128)(2,1)}) fusion(f32[8,8,64,512]{3,2,1,0:T(8,128)} %fusion.93, pred[8,512]{1,0:T(8,128)(4,1)S(1)} %or_and_fusion.2), kind=kOutput, calls=%fused_computation.111.clone.1 | output fusion | flops 16777728 | bytes 12603392 | tf_op jit(solution)/shard_map/while/body/eval_jaxpr/sub | solution.py:169
  725.6 2.5 broadcast_dynamic-update-slice_fusion.4
  728.1 8.8 copy.126
  736.9 6.6 fusion.97
  743.5 1.7 copy.129
  750.6 2.5 copy.92
  753.1 16.1 %fusion.45 = f32[1024,4096]{1,0:T(8,128)} fusion(bf16[1024,4096]{1,0:T(8,128)(2,1)} %param.19, bf16[896,1024]{0,1:T(8,128)(2,1)} %copy.92, bf16[128,1024]{0,1:T(8,128)(2,1)S(1)} %bitcast_select_fusion), kind=kOutput, calls=%fused_computation.77 | convolution fusion | flops 8594128896 | bytes 27262976 | tf_op jit(solution)/shard_map/dot_general | solution.py:190
  769.3 125.2 %reduce-scatter.2.cloned.1.call-done = f32[256,4096]{1,0:T(8,128)} async-done(((f32[1024,4096]{1,0:T(8,128)}), f32[256,4096]{1,0:T(8,128)}) %reduce-scatter.2.cloned.1.call-update) | async-done | bytes 4194320 | tf_op jit(solution)/shard_map/reduce_scatter | solution.py:189
  894.5 3.8 convert_element_type.51
  (107 shorter events, 42.6 us)
Async XLA Ops:
  22.5 7.3 copy-start
  230.5 6.2 slice-start
  230.5 352.1 %all-to-all-start.2 = ((bf16[8,8,64,1024]{3,2,1,0:T(8,128)(2,1)}), bf16[8,8,64,1024]{3,2,1,0:T(8,128)(2,1)}, u32[]{:S(2)}, u32[]{:S(2)}) async-start(bf16[8,8,64,1024]{3,2,1,0:T(8,128)(2,1)} %get-tuple-element.474), calls=%async_computation.2 | async-start | bytes 16777216 | tf_op jit(solution)/shard_map/all_to_all | solution.py:75
  235.7 231.1 %all-reduce.2.cloned.1.call-start = ((), (), s32[]{:S(2)}) async-start(), calls=%async_computation.4 | async-start | bytes 1572864 | tf_op jit(solution)/shard_map/psum | solution.py:29
  238.3 322.9 %all-gather.5.cloned.1.call-start = ((), (), s32[]{:S(2)}) async-start(), calls=%async_computation.6 | async-start | bytes 4718592 | tf_op jit(solution)/shard_map/all_gather | solution.py:33
  466.8 4.1 copy-start.2
  469.0 1.9 copy-start.3
  473.0 421.5 %reduce-scatter.2.cloned.1.call-start = ((), (), s32[]{:S(2)}) async-start(), calls=%async_computation.5 | async-start | bytes 20971520 | tf_op jit(solution)/shard_map/reduce_scatter | solution.py:189
  474.1 15.4 %collective-permute-start = (bf16[1,2,64,1024]{3,2,1,0:T(8,128)(2,1)S(1)}, bf16[1,2,64,1024]{3,2,1,0:T(8,128)(2,1)S(1)}, u32[]{:S(2)}, u32[]{:S(2)}) collective-permute-start(bf16[1,2,64,1024]{3,2,1,0:T(8,128)(2,1)S(1)} %maximum_bitcast_fusion), channel_id=1, source_target_pairs={{0,4},{4,8},{8,12},{12,16},{16,20},{20,24},{24,28},{1,5},{5,9},{9,... | collective-permute-start | bytes 786440 | tf_op jit(solution)/shard_map/ppermute | solution.py:21
  476.8 13.6 %collective-permute-start.1 = (bf16[1,2,64,1024]{3,2,1,0:T(8,128)(2,1)S(1)}, bf16[1,2,64,1024]{3,2,1,0:T(8,128)(2,1)S(1)}, u32[]{:S(2)}, u32[]{:S(2)}) collective-permute-start(bf16[1,2,64,1024]{3,2,1,0:T(8,128)(2,1)S(1)} %maximum_bitcast_fusion.1), channel_id=1, source_target_pairs={{4,0},{8,4},{12,8},{16,12},{20,16},{24,20},{28,24},{5,1},{9,5},{13... | collective-permute-start | bytes 786440 | tf_op jit(solution)/shard_map/ppermute | solution.py:22
  478.1 14.2 %copy-start.1 = (bf16[1024,1024]{1,0:T(8,128)(2,1)S(1)}, bf16[1024,1024]{1,0:T(8,128)(2,1)}, u32[]{:S(2)}) copy-start(bf16[1024,1024]{1,0:T(8,128)(2,1)} %param.15) | copy-start | bytes 6291460
  478.1 15.9 %copy-start.4 = (f32[8,128,1024]{2,1,0:T(8,128)S(1)}, f32[8,128,1024]{2,1,0:T(8,128)}, u32[]{:S(2)}) copy-start(f32[8,128,1024]{2,1,0:T(8,128)} %copy-done.3) | copy-start | bytes 12582916
  621.8 8.9 copy-start.5
  695.0 8.9 copy-start.5
  747.8 5.3 copy-start.6
Sparse Core Ops, SparseCore 0:
  239.9 226.8 all-reduce.1
  473.1 75.0 all-gather.4
  769.4 125.0 reduce-scatter.1
where the time goes:
time: 906 us; the launch traced here: 905 us
  waiting for transfers between devices  366 us (40%)
  blocking collectives  264 us (29%)
  local copies, waits for them, and re-layouts  135 us (15%)
  other arithmetic  64.4 us (7%)
  matrix products  51.6 us (6%)
  between operations  13.4 us (1%)
  starting transfers between devices  9.2 us (1%)
    psum x1, waiting for transfers between devices, from_root(): return lax.psum(block, axis)  228 us
    all_to_all x1, blocking collectives, local(): lax.all_to_all(sent_values, 'seq', split_axis=0, concat_axis=0, tiled=True)  186 us
    reduce_scatter x1, waiting for transfers between devices, local(): lax.psum_scatter(jnp.dot(attention, output_weight, preferred_element_type...  125 us
    while x24, local copies, waits for them, and re-layouts  69.2 us
    all_gather x2, blocking collectives, combined_all(): everything = jax.tree.map(lambda part: lax.all_gather(part, axis), array)  64.6 us
    sub x2, other arithmetic, attend(): block_scores - block_max  23 us
    dot_general x2, matrix products, attend(): jnp.einsum('bqhd,bkhd->bhqk', query_heads, group_keys, preferred_element_...  19.3 us
  transfers between devices with their start and end apart: 6, of which 4 were waited for; matrix products, arithmetic and copies ran while one was open for 4% of the time, Pallas kernels for 0%

commit v1 on v0

--- a/solution.py
+++ b/solution.py
@@ -9,6 +9,30 @@
 RANDOM = 3
 GLOBAL = 128
 masked_score = -1e30
+
+
+def split_up(value, dim, length):
+    lengths = value.shape
+    pieces = value.reshape(*lengths[:dim], length, lengths[dim] // length, *lengths[dim + 1 :])
+    return jnp.moveaxis(pieces, dim, 0)
+
+
+def in_order(tiles, dim):
+    tiles = jnp.moveaxis(tiles, 0, dim)
+    shape = tiles.shape
+    return tiles.reshape(*shape[:dim], shape[dim] * shape[dim + 1], *shape[dim + 2 :])
+
+
+def sent_to_each(x, axis, split_dim, concat_dim):
+    size, index = (lax.axis_size(axis), lax.axis_index(axis))
+    blocks = split_up(x, split_dim, size)
+    out = blocks
+    for step in range(1, size):
+        target, source = ((index + step) % size, (index - step) % size)
+        sent = lax.dynamic_index_in_dim(blocks, target, 0)
+        theirs = lax.ppermute(sent, axis, [(i, (i + step) % size) for i in range(size)])
+        out = lax.dynamic_update_slice_in_dim(out, theirs, source, axis=0)
+    return in_order(out, concat_dim)
 
 
 def padded(array, sides, width):
@@ -73,7 +97,7 @@
     sent_keys = jnp.take(key_blocks, wanted, axis=0)
     sent_values = jnp.take(value_blocks, wanted, axis=0)
     got_keys = lax.all_to_all(sent_keys, "seq", split_axis=0, concat_axis=0, tiled=True)
-    got_values = lax.all_to_all(sent_values, "seq", split_axis=0, concat_axis=0, tiled=True)
+    got_values = sent_to_each(sent_values, "seq", 0, 0)
     slot_width = slot_count + edge_slots
     flat_slots = owner_flat * slot_width + slot_ids
     random_keys = jnp.take(got_keys.reshape(-1, BLOCK, width_here), flat_slots, axis=0)

time: 906 us -> 953 us (1.052)
  blocking collectives: 264 us -> 233 us
  starting transfers between devices: 9.2 us -> 36.3 us
  local copies, waits for them, and re-layouts: 135 us -> 160 us
  waiting for transfers between devices: 366 us -> 387 us
    all_to_all x1 -> x0, blocking collectives: 186 us -> none  [local(): lax.all_to_all(sent_values, 'seq', split_axis=0, concat_axis=0, tiled=True)]
    all_gather x2, blocking collectives: 64.6 us -> 219 us  [combined_all(): everything = jax.tree.map(lambda part: lax.all_gather(part, axis), array)]
    ppermute x0 -> x7, starting transfers between devices: none -> 27.1 us  [sent_to_each(): lax.ppermute(sent, axis, [(i, (i + step) % size) for i in range(size)])]
    ppermute x0 -> x7, waiting for transfers between devices: none -> 21.2 us  [sent_to_each(): lax.ppermute(sent, axis, [(i, (i + step) % size) for i in range(size)])]
    dynamic_update_slice x0 -> x7, local copies, waits for them, and re-layouts: none -> 16 us  [sent_to_each(): out = lax.dynamic_update_slice_in_dim(out, theirs, source, axis=0)]
    ppermute x1, waiting for transfers between devices: 11.4 us -> 0.01 us  [padded(): before = lax.ppermute(last, axis, up)]
    ppermute x1, waiting for transfers between devices: 0.85 us -> 10.5 us  [padded(): after = lax.ppermute(first, axis, down)]
  transfers between devices with their start and end apart: 6 -> 13, of which waited for: 4 -> 5; matrix products, arithmetic and copies ran while one was open for 4% -> 6% of each run, Pallas kernels for 0% -> 0%
where the time goes in v1:
time: 953 us; the launch traced here: 951 us
  waiting for transfers between devices  387 us (41%)
  blocking collectives  233 us (24%)
  local copies, waits for them, and re-layouts  160 us (17%)
  other arithmetic  68.4 us (7%)
  matrix products  51.6 us (5%)
  starting transfers between devices  36.3 us (4%)
  between operations  13.6 us (1%)
    psum x1, waiting for transfers between devices, from_root(): return lax.psum(block, axis)  228 us
    all_gather x2, blocking collectives, combined_all(): everything = jax.tree.map(lambda part: lax.all_gather(part, axis), array)  219 us
    reduce_scatter x1, waiting for transfers between devices, local(): lax.psum_scatter(jnp.dot(attention, output_weight, preferred_element_type...  127 us
    while x24, local copies, waits for them, and re-layouts  69.3 us
    ppermute x7, starting transfers between devices, sent_to_each(): lax.ppermute(sent, axis, [(i, (i + step) % size) for i in range(size)])  27.1 us
    sub x2, other arithmetic, attend(): block_scores - block_max  23 us
    ppermute x7, waiting for transfers between devices, sent_to_each(): lax.ppermute(sent, axis, [(i, (i + step) % size) for i in range(size)])  21.2 us
    dot_general x2, matrix products, attend(): jnp.einsum('bqhd,bkhd->bhqk', query_heads, group_keys, preferred_element_...  19.3 us
  transfers between devices with their start and end apart: 13, of which 5 were waited for; matrix products, arithmetic and copies ran while one was open for 6% of the time, Pallas kernels for 0%

profile of v1, /device:TPU:0, one launch (start us, length us, event | category | flops | bytes accessed | tf_op | source)
XLA Modules:
  0.0 951.3 jit_solution(9368376471155318311)
XLA Ops:
  8.9 13.6 %all_to_all.17 = s32[8,1,8]{2,1,0:T(1,128)S(1)} all-to-all(s32[8,1,8]{2,1,0:T(1,128)S(1)} %bitcast.228), channel_id=1, replica_groups=mesh['seq'=8,'head'=4] {'seq'}, dimensions={0} | all-to-all | bytes 512 | tf_op jit(solution)/shard_map/all_to_all | solution.py:96
  22.6 7.3 gather_fusion
  29.8 5.5 gather_fusion.2
  35.4 11.8 %broadcast_select_fusion = (bf16[8,8,64,1024]{3,2,1,0:T(8,128)(2,1)}, bf16[8,8,64,1024]{3,2,1,0:T(8,128)(2,1)}) fusion(bf16[8,8,64,1024]{3,2,1,0:T(8,128)(2,1)} %bitcast.215, pred[8,8]{1,0:T(8,128)(4,1)S(1)} %compare_and_fusion, bf16[8,8,64,1024]{3,2,1,0:T(8,128)(2,1)} %bitcast.214), kind=kLoop, calls=%fused_computation.61 | loop fusion | flops 8388608 | bytes 33554496 | tf_op jit(solution)/shard_map/jit(_take)/select_n | solution.py:97
  47.2 5.2 all-to-all-start.1
  55.0 228.3 %all-reduce.2.cloned.1.call-done = bf16[3,128,1024]{1,2,0:T(8,128)(2,1)} async-done(((bf16[3,128,1024]{1,2,0:T(8,128)(2,1)}), bf16[3,128,1024]{1,2,0:T(8,128)(2,1)}) %all-reduce.2.cloned.1.call-update) | async-done | bytes 786448 | tf_op jit(solution)/shard_map/psum | solution.py:53
  291.5 2.6 collective-permute-start
  294.2 6.3 dynamic-slice_bitcast_fusion.6
  303.2 3.6 collective-permute-start.3
  310.0 10.5 %collective-permute-done.1 = bf16[1,2,64,1024]{3,2,1,0:T(8,128)(2,1)S(1)} collective-permute-done((bf16[1,2,64,1024]{3,2,1,0:T(8,128)(2,1)S(1)}, bf16[1,2,64,1024]{3,2,1,0:T(8,128)(2,1)S(1)}, u32[]{:S(2)}, u32[]{:S(2)}) %collective-permute-start.1) | collective-permute-done | bytes 262176 | tf_op jit(solution)/shard_map/ppermute | solution.py:46
  323.8 19.9 %collective-permute-done.2 = bf16[1,1,8,64,1024]{4,3,2,0,1:T(8,128)(2,1)} collective-permute-done((bf16[1,1,8,64,1024]{4,3,2,0,1:T(8,128)(2,1)}, bf16[1,1,8,64,1024]{4,3,2,0,1:T(8,128)(2,1)}, u32[]{:S(2)}, u32[]{:S(2)}) %collective-permute-start.2) | collective-permute-done | bytes 1048608 | tf_op jit(solution)/shard_map/ppermute | solution.py:33
  344.0 3.3 pad_maximum_fusion.1
  348.5 17.5 %collective-permute-start.8 = (bf16[1,1,8,64,1024]{4,3,2,0,1:T(8,128)(2,1)S(1)}, bf16[1,1,8,64,1024]{4,3,2,0,1:T(8,128)(2,1)}, u32[]{:S(2)}, u32[]{:S(2)}) collective-permute-start(bf16[1,1,8,64,1024]{4,3,2,0,1:T(8,128)(2,1)S(1)} %get-tuple-element.463), channel_id=1, source_target_pairs={{0,28},{4,0},{8,4},{12,8},{16,12},{20,16},{24,20},{28,24},{1,29},{... | collective-permute-start | bytes 3145736 | tf_op jit(solution)/shard_map/ppermute | solution.py:33
  367.0 188.5 %all-gather.1 = f32[64,128]{1,0:T(8,128)S(1)} all-gather(f32[8,128]{1,0:T(8,128)S(1)} %fusion.37), channel_id=3, replica_groups=mesh['seq'=8,'head'=4] {'seq'}, dimensions={0}, use_global_device_ids=true | all-gather | bytes 36864 | tf_op jit(solution)/shard_map/all_gather | solution.py:57
  555.4 31.0 %all-gather = f32[64,128]{1,0:T(8,128)S(1)} all-gather(f32[8,128]{1,0:T(8,128)S(1)} %get-tuple-element.487), channel_id=2, replica_groups=mesh['seq'=8,'head'=4] {'seq'}, dimensions={0}, use_global_device_ids=true | all-gather | bytes 36864 | tf_op jit(solution)/shard_map/all_gather | solution.py:57
  590.1 2.3 constant_dynamic-update-slice_fusion.7
  592.4 2.3 constant_dynamic-update-slice_fusion.6
  594.7 2.3 constant_dynamic-update-slice_fusion.5
  597.0 2.3 constant_dynamic-update-slice_fusion.4
  599.2 2.3 constant_dynamic-update-slice_fusion.3
  601.5 2.3 constant_dynamic-update-slice_fusion.2
  603.8 2.3 constant_dynamic-update-slice_fusion.1
  606.1 8.4 gather_fusion.1
  615.6 11.0 %while.33 = (s32[]{:T(128)}, f32[8,128]{1,0:T(8,128)S(1)}, f32[8,128]{1,0:T(8,128)S(1)}, f32[8,128,128]{2,1,0:T(8,128)S(1)}, f32[8,8,128]{2,1,0:T(8,128)S(1)}, /...) while((s32[]{:T(128)}, f32[8,128]{1,0:T(8,128)S(1)}, ...), condition=%wide.region_4.5_spmd, body=%wide.region_3.4_spmd.sunk | while | flops 399365 | bytes 1613975 | solution.py:63
  627.5 8.4 gather_fusion.3
  635.9 10.4 %broadcast_select_fusion.2 = (bf16[48,64,1024]{2,1,0:T(8,128)(2,1)}, bf16[48,64,1024]{2,1,0:T(8,128)(2,1)}) fusion(bf16[48,64,1024]{2,1,0:T(8,128)(2,1)} %gather_fusion.3, pred[48]{0:T(512)(128)(4,1)S(1)} %get-tuple-element.453, bf16[48,64,1024]{2,1,0:T(8,128)(2,1)} %gather_fusion.1), kind=kLoop, calls=%fused_computation.63 | loop fusion | flops 6291456 | bytes 25165872 | tf_op jit(solution)/shard_map/jit(_take)/select_n | solution.py:103
  646.3 146.6 %while.34 = (s32[]{:T(128)}, bf16[2,512,1024]{2,1,0:T(8,128)(2,1)}, s32[2]{0:T(128)S(1)}, bf16[18,64,1024]{2,1,0:T(8,128)(2,1)S(1)}, bf16[2,8,3,64,1024]{4,3,2,1...) while((s32[]{:T(128)}, bf16[2,512,1024]{2,1,0:T(8,128)(2,1)}, ...), condition=%wide.region_11.14_spmd.clone.clone, body=%wide.region_8.13_spmd.clone.clone.sunk | while | flops 1091585536 | bytes 126397792 | solution.py:208
  653.0 2.3 fusion.88
  657.5 6.7 bitcast_dynamic-update-slice_fusion.3
  664.2 2.5 broadcast_dynamic-update-slice_fusion.5
  666.8 8.9 copy.127
  676.1 9.7 %fusion.93 = f32[8,8,64,512]{3,2,1,0:T(8,128)} fusion(bf16[8,512,8,128]{3,2,1,0:T(8,128)(2,1)} %bitcast.201, bf16[8,64,8,128]{3,2,1,0:T(8,128)(2,1)S(1)} %bitcast.204), kind=kOutput, calls=%fused_computation.16.clone.1 | convolution fusion | flops 536870912 | bytes 17825792 | tf_op jit(solution)/shard_map/while/body/eval_jaxpr/bqhd,bkhd->bhqk/dot_general | solution.py:181
  685.9 11.5 %fusion.96 = (f32[8,8,64]{2,1,0:T(8,128)S(1)}, bf16[8,8,64,512]{3,2,1,0:T(8,128)(2,1)}) fusion(f32[8,8,64,512]{3,2,1,0:T(8,128)} %fusion.93, pred[8,512]{1,0:T(8,128)(4,1)S(1)} %or_and_fusion.2), kind=kOutput, calls=%fused_computation.125.clone.1 | output fusion | flops 16777728 | bytes 12603392 | tf_op jit(solution)/shard_map/while/body/eval_jaxpr/sub | solution.py:193
  697.4 2.5 broadcast_dynamic-update-slice_fusion.4
  699.9 8.8 copy.126
  708.7 6.6 fusion.97
  730.8 6.7 bitcast_dynamic-update-slice_fusion.3
  737.5 2.5 broadcast_dynamic-update-slice_fusion.5
  740.1 8.9 copy.127
  749.4 9.7 %fusion.93 = f32[8,8,64,512]{3,2,1,0:T(8,128)} fusion(bf16[8,512,8,128]{3,2,1,0:T(8,128)(2,1)} %bitcast.201, bf16[8,64,8,128]{3,2,1,0:T(8,128)(2,1)S(1)} %bitcast.204), kind=kOutput, calls=%fused_computation.16.clone.1 | convolution fusion | flops 536870912 | bytes 17825792 | tf_op jit(solution)/shard_map/while/body/eval_jaxpr/bqhd,bkhd->bhqk/dot_general | solution.py:181
  759.2 11.5 %fusion.96 = (f32[8,8,64]{2,1,0:T(8,128)S(1)}, bf16[8,8,64,512]{3,2,1,0:T(8,128)(2,1)}) fusion(f32[8,8,64,512]{3,2,1,0:T(8,128)} %fusion.93, pred[8,512]{1,0:T(8,128)(4,1)S(1)} %or_and_fusion.2), kind=kOutput, calls=%fused_computation.125.clone.1 | output fusion | flops 16777728 | bytes 12603392 | tf_op jit(solution)/shard_map/while/body/eval_jaxpr/sub | solution.py:193
  770.7 2.5 broadcast_dynamic-update-slice_fusion.4
  773.2 8.8 copy.126
  782.0 6.6 fusion.97
  795.7 2.5 copy.92
  798.3 16.1 %fusion.45 = f32[1024,4096]{1,0:T(8,128)} fusion(bf16[1024,4096]{1,0:T(8,128)(2,1)} %param.19, bf16[896,1024]{0,1:T(8,128)(2,1)} %copy.92, bf16[128,1024]{0,1:T(8,128)(2,1)S(1)} %bitcast_select_fusion), kind=kOutput, calls=%fused_computation.77 | convolution fusion | flops 8594128896 | bytes 27262976 | tf_op jit(solution)/shard_map/dot_general | solution.py:214
  814.4 126.5 %reduce-scatter.2.cloned.1.call-done = f32[256,4096]{1,0:T(8,128)} async-done(((f32[1024,4096]{1,0:T(8,128)}), f32[256,4096]{1,0:T(8,128)}) %reduce-scatter.2.cloned.1.call-update) | async-done | bytes 4194320 | tf_op jit(solution)/shard_map/reduce_scatter | solution.py:213
  940.9 3.8 convert_element_type.51
  (126 shorter events, 72.1 us)
Async XLA Ops:
  22.5 7.3 copy-start
  47.2 6.2 slice-start
  47.2 580.3 %all-to-all-start.1 = ((bf16[8,8,64,1024]{3,2,1,0:T(8,128)(2,1)}), bf16[8,8,64,1024]{3,2,1,0:T(8,128)(2,1)}, u32[]{:S(2)}, u32[]{:S(2)}) async-start(bf16[8,8,64,1024]{3,2,1,0:T(8,128)(2,1)} %get-tuple-element.481), calls=%async_computation.1 | async-start | bytes 16777216 | tf_op jit(solution)/shard_map/all_to_all | solution.py:99
  52.3 231.0 %all-reduce.2.cloned.1.call-start = ((), (), s32[]{:S(2)}) async-start(), calls=%async_computation.3 | async-start | bytes 1572864 | tf_op jit(solution)/shard_map/psum | solution.py:53
  54.9 559.5 %all-gather.5.cloned.1.call-start = ((), (), s32[]{:S(2)}) async-start(), calls=%async_computation.5 | async-start | bytes 4718592 | tf_op jit(solution)/shard_map/all_gather | solution.py:57
  283.3 5.0 copy-start.1
  286.3 2.0 copy-start.2
  290.4 650.6 %reduce-scatter.2.cloned.1.call-start = ((), (), s32[]{:S(2)}) async-start(), calls=%async_computation.4 | async-start | bytes 20971520 | tf_op jit(solution)/shard_map/reduce_scatter | solution.py:213
  291.5 16.6 %collective-permute-start = (bf16[1,2,64,1024]{3,2,1,0:T(8,128)(2,1)S(1)}, bf16[1,2,64,1024]{3,2,1,0:T(8,128)(2,1)S(1)}, u32[]{:S(2)}, u32[]{:S(2)}) collective-permute-start(bf16[1,2,64,1024]{3,2,1,0:T(8,128)(2,1)S(1)} %maximum_bitcast_fusion), channel_id=1, source_target_pairs={{0,4},{4,8},{8,12},{12,16},{16,20},{20,24},{24,28},{1,5},{5,9},{9,... | collective-permute-start | bytes 786440 | tf_op jit(solution)/shard_map/ppermute | solution.py:45
  300.5 43.2 %collective-permute-start.2 = (bf16[1,1,8,64,1024]{4,3,2,0,1:T(8,128)(2,1)}, bf16[1,1,8,64,1024]{4,3,2,0,1:T(8,128)(2,1)}, u32[]{:S(2)}, u32[]{:S(2)}) collective-permute-start(bf16[1,1,8,64,1024]{4,3,2,0,1:T(8,128)(2,1)} %get-tuple-element.469), channel_id=1, source_target_pairs={{0,4},{4,8},{8,12},{12,16},{16,20},{20,24},{24,28},{28,0},{1,5},{5... | collective-permute-start | bytes 3145736 | tf_op jit(solution)/shard_map/ppermute | solution.py:33
  301.9 18.6 %collective-permute-start.1 = (bf16[1,2,64,1024]{3,2,1,0:T(8,128)(2,1)S(1)}, bf16[1,2,64,1024]{3,2,1,0:T(8,128)(2,1)S(1)}, u32[]{:S(2)}, u32[]{:S(2)}) collective-permute-start(bf16[1,2,64,1024]{3,2,1,0:T(8,128)(2,1)S(1)} %maximum_bitcast_fusion.1), channel_id=1, source_target_pairs={{4,0},{8,4},{12,8},{16,12},{20,16},{24,20},{28,24},{5,1},{9,5},{13... | collective-permute-start | bytes 786440 | tf_op jit(solution)/shard_map/ppermute | solution.py:46
  303.2 45.4 %collective-permute-start.3 = (bf16[1,1,8,64,1024]{4,3,2,0,1:T(8,128)(2,1)}, bf16[1,1,8,64,1024]{4,3,2,0,1:T(8,128)(2,1)}, u32[]{:S(2)}, u32[]{:S(2)}) collective-permute-start(bf16[1,1,8,64,1024]{4,3,2,0,1:T(8,128)(2,1)} %get-tuple-element.468), channel_id=1, source_target_pairs={{0,8},{4,12},{8,16},{12,20},{16,24},{20,28},{24,0},{28,4},{1,9},{5... | collective-permute-start | bytes 3145736 | tf_op jit(solution)/shard_map/ppermute | solution.py:33
  307.0 59.0 %copy-start.3 = (f32[8,128,1024]{2,1,0:T(8,128)S(1)}, f32[8,128,1024]{2,1,0:T(8,128)}, u32[]{:S(2)}) copy-start(f32[8,128,1024]{2,1,0:T(8,128)} %copy-done.2) | copy-start | bytes 12582916
  307.0 287.7 %collective-permute-start.4 = (bf16[1,1,8,64,1024]{4,3,2,0,1:T(8,128)(2,1)}, bf16[1,1,8,64,1024]{4,3,2,0,1:T(8,128)(2,1)}, u32[]{:S(2)}, u32[]{:S(2)}) collective-permute-start(bf16[1,1,8,64,1024]{4,3,2,0,1:T(8,128)(2,1)} %get-tuple-element.467), channel_id=1, source_target_pairs={{0,12},{4,16},{8,20},{12,24},{16,28},{20,0},{24,4},{28,8},{1,13},{... | collective-permute-start | bytes 3145736 | tf_op jit(solution)/shard_map/ppermute | solution.py:33
  308.1 288.9 %collective-permute-start.5 = (bf16[1,1,8,64,1024]{4,3,2,0,1:T(8,128)(2,1)}, bf16[1,1,8,64,1024]{4,3,2,0,1:T(8,128)(2,1)}, u32[]{:S(2)}, u32[]{:S(2)}) collective-permute-start(bf16[1,1,8,64,1024]{4,3,2,0,1:T(8,128)(2,1)} %get-tuple-element.466), channel_id=1, source_target_pairs={{0,16},{4,20},{8,24},{12,28},{16,0},{20,4},{24,8},{28,12},{1,17},{... | collective-permute-start | bytes 3145736 | tf_op jit(solution)/shard_map/ppermute | solution.py:33
  320.4 278.8 %collective-permute-start.6 = (bf16[1,1,8,64,1024]{4,3,2,0,1:T(8,128)(2,1)}, bf16[1,1,8,64,1024]{4,3,2,0,1:T(8,128)(2,1)}, u32[]{:S(2)}, u32[]{:S(2)}) collective-permute-start(bf16[1,1,8,64,1024]{4,3,2,0,1:T(8,128)(2,1)} %get-tuple-element.465), channel_id=1, source_target_pairs={{0,20},{4,24},{8,28},{12,0},{16,4},{20,8},{24,12},{28,16},{1,21},{... | collective-permute-start | bytes 3145736 | tf_op jit(solution)/shard_map/ppermute | solution.py:33
  343.7 257.9 %collective-permute-start.7 = (bf16[1,1,8,64,1024]{4,3,2,0,1:T(8,128)(2,1)}, bf16[1,1,8,64,1024]{4,3,2,0,1:T(8,128)(2,1)}, u32[]{:S(2)}, u32[]{:S(2)}) collective-permute-start(bf16[1,1,8,64,1024]{4,3,2,0,1:T(8,128)(2,1)} %get-tuple-element.464), channel_id=1, source_target_pairs={{0,24},{4,28},{8,0},{12,4},{16,8},{20,12},{24,16},{28,20},{1,25},{... | collective-permute-start | bytes 3145736 | tf_op jit(solution)/shard_map/ppermute | solution.py:33
  348.5 255.3 %collective-permute-start.8 = (bf16[1,1,8,64,1024]{4,3,2,0,1:T(8,128)(2,1)S(1)}, bf16[1,1,8,64,1024]{4,3,2,0,1:T(8,128)(2,1)}, u32[]{:S(2)}, u32[]{:S(2)}) collective-permute-start(bf16[1,1,8,64,1024]{4,3,2,0,1:T(8,128)(2,1)S(1)} %get-tuple-element.463), channel_id=1, source_target_pairs={{0,28},{4,0},{8,4},{12,8},{16,12},{20,16},{24,20},{28,24},{1,29},{... | collective-permute-start | bytes 3145736 | tf_op jit(solution)/shard_map/ppermute | solution.py:33
  666.8 8.9 copy-start.4
  740.1 8.9 copy-start.4
  792.9 5.3 copy-start.5
Sparse Core Ops, SparseCore 0:
  56.6 226.7 all-reduce.1
  290.5 202.8 all-gather.4
  814.5 126.3 reduce-scatter.1
